TPU v7x, 8 devices: a whole 2x2x1 slice. The times are simulated.
8 devices in a mesh: dp: 1 (over z), cy: 2 (over y), cx: 2 (over x), core: 2 (over core).
Axes of the slice: x: 2, y: 2, z: 1, core: 2. Of those that a mesh axis runs over, the one named last changes fastest.
Arguments:
- x_in: bfloat16 [1, 1024, 2048], P('dp', ('cy', 'cx', 'core'))
- w_qkv: bfloat16 [2048, 40, 64], replicated
- w_out: bfloat16 [32, 64, 2048], replicated
Outputs:
- output: bfloat16 [1, 1024, 2048], P('dp', ('cy', 'cx', 'core'))
All inputs are finite; a program needn't handle non-finite values.
Results may differ from a plain program's by a relative error of at most 0.00798741.
Values are sent between devices in bfloat16 or wider.
A program may use at most 1 GiB of HBM per device.

v0:
```python
import jax
import jax.numpy as jnp
from jax import lax
from jax.sharding import PartitionSpec as P


def solution(mesh):
    cy_size = mesh.shape["cy"]
    head_split = mesh.shape["cx"] * mesh.shape["core"]
    seq_spec = P("dp", ("cy", "cx", "core"))

    def local_layer(x_loc, w_qkv, w_out):
        num_heads = w_out.shape[0]
        head_dim = w_out.shape[1]
        num_kv = (w_qkv.shape[1] - num_heads) // 2
        num_tokens = x_loc.shape[1]
        kv_slots = max(num_kv, head_split)
        repeat_kv = kv_slots // num_kv
        q_local = num_heads // head_split
        kv_local = kv_slots // head_split
        group_size = q_local // kv_local
        qkv_rows = jnp.einsum("sc,chd->shd", x_loc[0], w_qkv, preferred_element_type=jnp.float32).astype(jnp.bfloat16)
        q_part = qkv_rows[:, :num_heads].reshape(num_tokens, head_split, q_local, head_dim)
        k_part = jnp.repeat(qkv_rows[:, num_heads:num_heads + num_kv], repeat_kv, axis=1).reshape(num_tokens, head_split, kv_local, head_dim)
        v_part = jnp.repeat(qkv_rows[:, num_heads + num_kv:], repeat_kv, axis=1).reshape(num_tokens, head_split, kv_local, head_dim)
        packed = jnp.concatenate([q_part, k_part, v_part], axis=2)
        packed = lax.all_to_all(packed, "cx", 1, 0, tiled=True)
        packed = lax.all_to_all(packed, "core", 1, 0, tiled=True)
        seq_len = packed.shape[0]
        queries = packed[:, 0, :q_local].reshape(seq_len, kv_local, group_size, head_dim)
        kv_all = lax.all_gather(packed[:, 0, q_local:], "cy")
        logit_scale = head_dim ** -0.5
        run_max = jnp.full((kv_local, group_size, seq_len), -jnp.inf, jnp.float32)
        run_sum = jnp.zeros((kv_local, group_size, seq_len), jnp.float32)
        accumulator = jnp.zeros((kv_local, group_size, seq_len, head_dim), jnp.float32)
        for block_idx in range(cy_size):
            k_block = kv_all[block_idx, :, :kv_local]
            v_block = kv_all[block_idx, :, kv_local:]
            scores = jnp.einsum("qkgd,skd->kgqs", queries, k_block, preferred_element_type=jnp.float32) * logit_scale
            new_max = jnp.maximum(run_max, scores.max(axis=-1))
            rescale = jnp.exp(run_max - new_max)
            weights = jnp.exp(scores - new_max[..., None])
            run_sum = run_sum * rescale + weights.sum(axis=-1)
            accumulator = accumulator * rescale[..., None] + jnp.einsum("kgqs,skd->kgqd", weights.astype(jnp.bfloat16), v_block, preferred_element_type=jnp.float32)
            run_max = new_max
        attn_out = (accumulator / run_sum[..., None]).astype(jnp.bfloat16)
        attn_out = jnp.transpose(attn_out, (2, 0, 1, 3)).reshape(seq_len, q_local, head_dim)
        attn_out = lax.all_to_all(attn_out, "core", 0, 1, tiled=True)
        attn_out = lax.all_to_all(attn_out, "cx", 0, 1, tiled=True)
        y_local = jnp.einsum("shd,hdc->sc", attn_out, w_out, preferred_element_type=jnp.float32)
        return y_local.astype(jnp.bfloat16)[None]

    return jax.shard_map(local_layer, mesh=mesh, in_specs=(seq_spec, P(), P()), out_specs=seq_spec, check_vma=False)
```

profile of v0, /device:TPU:0, one launch (start us, length us, event | category | flops | bytes accessed | tf_op | source)
XLA Modules:
  0.0 69.6 jit_solution(3675251464560125042)
XLA Ops:
  0.0 0.0 copy-start
  0.0 1.0 %copy-done = bf16[1,128,2048]{2,1,0:T(8,128)(2,1)S(1)} copy-done((bf16[1,128,2048]{2,1,0:T(8,128)(2,1)S(1)}, bf16[1,128,2048]{2,1,0:T(8,128)(2,1)}, u32[]{:S(2)}) %copy-start) | copy-done | bytes 524312
  1.0 5.6 %fusion.32 = f32[128,2560]{0,1:S(1)} fusion(bf16[2048,2560]{0,1:T(8,128)(2,1)} %bitcast.139, bf16[1,128,2048]{2,1,0:T(8,128)(2,1)S(1)} %copy-done), kind=kOutput, calls=%fused_computation.29 | convolution fusion | flops 1342177280 | bytes 12320768
  6.7 0.1 convert_element_type.18
  6.8 0.1 pad_maximum_fusion
  6.9 13.8 %all_to_all.72 = bf16[128,4,10,64]{0,3,2,1:T(8,128)(2,1)S(1)} all-to-all(bf16[128,4,10,64]{0,3,2,1:T(8,128)(2,1)S(1)} %pad_maximum_fusion), channel_id=1, replica_groups=mesh['dp'=1,'cy'=2,'cx'=2,'core'=2] {'cx'}, dimensions={1} | all-to-all | bytes 1310720 | tf_op jit(solution)/shard_map/all_to_all | solution.py:27
  20.7 0.7 copy.77
  21.4 0.4 all_to_all.55
  21.8 4.3 %all_to_all.73 = bf16[256,2,10,64]{0,3,2,1:T(8,128)(2,1)S(1)} all-to-all(bf16[256,2,10,64]{0,3,2,1:T(8,128)(2,1)S(1)} %all_to_all.55), channel_id=1, replica_groups=mesh['dp'=1,'cy'=2,'cx'=2,'core'=2] {'core'}, dimensions={1} | all-to-all | bytes 1310720 | tf_op jit(solution)/shard_map/all_to_all | solution.py:28
  26.2 6.2 %all-gather = bf16[1024,1,2,64]{0,3,2,1:T(8,128)(2,1)S(1)} all-gather(bf16[512,1,2,64]{0,3,2,1:T(8,128)(2,1)S(1)} %slice.39), channel_id=2, replica_groups=mesh['dp'=1,'cy'=2,'cx'=2,'core'=2] {'cy'}, dimensions={0}, use_global_device_ids=true | all-gather | bytes 393216 | tf_op jit(solution)/shard_map/all_gather | solution.py:31
  32.4 0.2 reshape.124
  32.5 0.4 fusion.38
  32.9 1.3 %bitcast_reduce_fusion = (f32[8,512]{1,0:T(8,128)S(1)}, f32[512,512,8]{1,0,2:T(8,128)S(1)}) fusion(bf16[512,1,10,64]{0,3,2,1:T(8,128)(2,1)S(1)} %bitcast.142, bf16[1,512,1,64]{1,0,3,2:T(2,128)(2,1)S(1)} %get-tuple-element.10), kind=kOutput, calls=%fused_computation.1 | convolution fusion | flops 272625664 | bytes 9060352 | tf_op jit(solution)/shard_map/qkgd,skd->kgqs/dot_general | solution.py:39
  34.2 1.3 %bitcast_reduce_fusion.1 = (f32[8,512]{1,0:T(8,128)S(1)}, f32[512,512,8]{1,0,2:T(8,128)S(1)}) fusion(bf16[512,1,10,64]{0,3,2,1:T(8,128)(2,1)S(1)} %bitcast.143, bf16[1,512,1,64]{1,0,3,2:T(2,128)(2,1)S(1)} %get-tuple-element.12), kind=kOutput, calls=%fused_computation.4 | convolution fusion | flops 272625664 | bytes 9060352 | tf_op jit(solution)/shard_map/qkgd,skd->kgqs/dot_general | solution.py:39
  35.5 2.8 %fusion.2 = (f32[8,512]{1,0:T(8,128)S(1)}, f32[8,512]{1,0:T(8,128)S(1)}) fusion(f32[512,512,8]{1,0,2:T(8,128)S(1)} %get-tuple-element.15, f32[8,512]{1,0:T(8,128)S(1)} %get-tuple-element.14, f32[8,512]{1,0:T(8,128)S(1)} %max.17, f32[512,512,8]{1,0,2:T(8,128)S(1)} %get-tuple-element.17), kind=kLoop, calls=%fused_computation.6 | loop fusion | flops 12574720 | bytes 16842752 | tf_op jit(solution)/shard_map/reduce_sum | solution.py:43
  38.4 1.6 %fusion.21 = f32[8,512,64]{1,2,0:T(8,128)S(1)} fusion(f32[512,512,8]{1,0,2:T(8,128)S(1)} %get-tuple-element.15, f32[8,512]{1,0:T(8,128)S(1)} %get-tuple-element.14, f32[8,512]{1,0:T(8,128)S(1)} %get-tuple-element.6, f32[8,512]{1,0:T(8,128)S(1)} %get-tuple-element.13, bf16[1,512,1,64]{1,0,3,2:T(2,128)(2,1)S(1)} %get-tuple-element.11), kind=kOutput, calls=%fused_computation.22 | convolution fusion | flops 275251200 | bytes 9551872 | tf_op jit(solution)/shard_map/kgqs,skd->kgqd/dot_general | solution.py:44
  40.0 1.6 %fusion.29 = bf16[512,8,64]{0,2,1:T(8,128)(2,1)S(1)} fusion(f32[8,512,64]{1,2,0:T(8,128)S(1)} %fusion.21, f32[512,512,8]{1,0,2:T(8,128)S(1)} %get-tuple-element.17, f32[8,512]{1,0:T(8,128)S(1)} %max.17, f32[8,512]{1,0:T(8,128)S(1)} %get-tuple-element.5, bf16[1,512,1,64]{1,0,3,2:T(2,128)(2,1)S(1)} %get-tuple-element.9), kind=kOutput, calls=%fused_computation.25 | convolution fusion | flops 275513344 | bytes 10059776 | tf_op jit(solution)/shard_map/kgqs,skd->kgqd/dot_general | solution.py:44
  41.6 0.8 %copy.48 = bf16[512,8,64]{2,1,0:T(8,128)(2,1)S(1)} copy(bf16[512,8,64]{0,2,1:T(8,128)(2,1)S(1)} %fusion.29) | data formatting | bytes 1048576 | tf_op jit(solution)/shard_map/reshape | solution.py:47
  42.4 0.8 %reshape.132 = bf16[2,2,65536]{2,1,0:T(2,128)(2,1)S(1)} reshape(bf16[512,8,64]{2,1,0:T(8,128)(2,1)S(1)} %copy.48) | data formatting | bytes 1048576
  43.3 4.2 %all_to_all.74 = bf16[2,2,65536]{2,1,0:T(2,128)(2,1)S(1)} all-to-all(bf16[2,2,65536]{2,1,0:T(2,128)(2,1)S(1)} %reshape.132), channel_id=1, replica_groups=mesh['dp'=1,'cy'=2,'cx'=2,'core'=2] {'core'}, dimensions={0} | all-to-all | bytes 1048576 | tf_op jit(solution)/shard_map/all_to_all | solution.py:48
  47.4 0.7 %reshape.133 = bf16[512,8,64]{2,1,0:T(8,128)(2,1)S(1)} reshape(bf16[2,2,65536]{2,1,0:T(2,128)(2,1)S(1)} %all_to_all.74) | data formatting | bytes 1048576
  48.1 1.0 %copy.56 = bf16[2,256,8,64]{1,0,3,2:T(2,128)(2,1)S(1)} copy(bf16[2,256,8,64]{3,2,1,0:T(8,128)(2,1)S(1)} %bitcast.144) | data formatting | bytes 1048576 | tf_op jit(solution)/shard_map/all_to_all | solution.py:48
  49.2 1.3 %copy.57 = bf16[256,2,8,64]{3,2,1,0:T(8,128)(2,1)S(1)} copy(bf16[256,2,8,64]{0,1,3,2:T(2,128)(2,1)S(1)} %bitcast.151) | data formatting | bytes 1048576 | tf_op jit(solution)/shard_map/all_to_all | solution.py:48
  50.5 0.8 %reshape.134 = bf16[2,2,65536]{2,1,0:T(2,128)(2,1)S(1)} reshape(bf16[256,16,64]{2,1,0:T(8,128)(2,1)S(1)} %bitcast.145) | data formatting | bytes 1048576
  51.3 11.0 %all_to_all.75 = bf16[2,2,65536]{2,1,0:T(2,128)(2,1)S(1)} all-to-all(bf16[2,2,65536]{2,1,0:T(2,128)(2,1)S(1)} %reshape.134), channel_id=1, replica_groups=mesh['dp'=1,'cy'=2,'cx'=2,'core'=2] {'cx'}, dimensions={0} | all-to-all | bytes 1048576 | tf_op jit(solution)/shard_map/all_to_all | solution.py:49
  62.4 0.7 %reshape.135 = bf16[256,16,64]{2,1,0:T(8,128)(2,1)S(1)} reshape(bf16[2,2,65536]{2,1,0:T(2,128)(2,1)S(1)} %all_to_all.75) | data formatting | bytes 1048576
  63.1 0.9 %copy.58 = bf16[2,128,16,64]{1,0,3,2:T(2,128)(2,1)S(1)} copy(bf16[2,128,16,64]{3,2,1,0:T(8,128)(2,1)S(1)} %bitcast.146) | data formatting | bytes 1048576 | tf_op jit(solution)/shard_map/all_to_all | solution.py:49
  64.0 0.1 copy.53
  64.1 5.5 %fusion.17 = bf16[1,128,2048]{2,1,0:T(8,128)(2,1)} fusion(bf16[128,32,64]{0,2,1:T(8,128)(2,1)S(1)} %bitcast.147, bf16[32,64,2048]{2,1,0:T(8,128)(2,1)} %param.5), kind=kOutput, calls=%fused_computation.20 | convolution fusion | flops 1074003968 | bytes 9437184 | tf_op jit(solution)/shard_map/shd,hdc->sc/dot_general | solution.py:50
  (6 shorter events, 0.1 us)
Async XLA Ops:
  0.0 1.0 %copy-start = (bf16[1,128,2048]{2,1,0:T(8,128)(2,1)S(1)}, bf16[1,128,2048]{2,1,0:T(8,128)(2,1)}, u32[]{:S(2)}) copy-start(bf16[1,128,2048]{2,1,0:T(8,128)(2,1)} %param.3) | copy-start | bytes 1572868
where the time goes:
time: 69.9 us; the launch traced here: 69.6 us
  blocking collectives  39.4 us (56%)
  matrix products  16.9 us (24%)
  local copies, waits for them, and re-layouts  10 us (14%)
  other arithmetic  3.06 us (4%)
    all_to_all x1, blocking collectives, local_layer(): packed = lax.all_to_all(packed, 'cx', 1, 0, tiled=True)  13.8 us
    all_to_all x1, blocking collectives, local_layer(): attn_out = lax.all_to_all(attn_out, 'cx', 0, 1, tiled=True)  11 us
    all_gather x1, blocking collectives, local_layer(): kv_all = lax.all_gather(packed[:, 0, q_local:], 'cy')  6.2 us
    unnamed x1, matrix products  5.61 us
    dot_general x1, matrix products, local_layer(): jnp.einsum('shd,hdc->sc', attn_out, w_out, preferred_element_type=jnp.flo...  5.47 us
    all_to_all x1, blocking collectives, local_layer(): packed = lax.all_to_all(packed, 'core', 1, 0, tiled=True)  4.26 us
    all_to_all x1, blocking collectives, local_layer(): attn_out = lax.all_to_all(attn_out, 'core', 0, 1, tiled=True)  4.16 us
    unnamed x6, local copies, waits for them, and re-layouts  4.16 us

commit v1 on v0

v1 whole, which is shorter than its diff:
```python
import functools
import math

import jax
import jax.numpy as jnp
from jax import lax
from jax.experimental import pallas as pl
from jax.experimental.pallas import tpu as pltpu
from jax.sharding import PartitionSpec as P

MESH = pl.DeviceIdType.MESH
F32 = jnp.float32
BF16 = jnp.bfloat16

TOK = 128
WIDTH = 2048
HEADS = 32
KVH = 4
HD = 64
NKV = KVH * HD
QROWS = HEADS * HD
TILES = HEADS // 2
COLS = 2 * TOK
QCHUNKS = 4
OCHUNKS = 4
SCALE = (HD ** -0.5) * math.log2(math.e)


def kernel(x_hbm, wt_hbm, wo_hbm, y_hbm,
           x_v, xt_v, wkv_v, wq_v, wo_v, qp_v, k_v, vt_v, m_v, l_v, o_v, ob_v, y_v,
           x_sem, wkv_sem, wq_sem, wo_sem, y_sem, send_sem, recv_sem):
    cy = lax.axis_index("cy")
    cx = lax.axis_index("cx")
    co = lax.axis_index("core")
    partner = {"core": 1 - co}
    xnbr = {"cx": 1 - cx}
    ynbr = {"cy": 1 - cy}

    x_copy = pltpu.make_async_copy(x_hbm.at[0], x_v, x_sem)
    x_copy.start()
    wkv_copies = []
    for i in range(2):
        c = pltpu.make_async_copy(wt_hbm.at[pl.ds(QROWS + i * NKV, NKV)], wkv_v.at[i], wkv_sem.at[i])
        c.start()
        wkv_copies.append(c)
    qstep = QROWS // QCHUNKS
    wq_copies = []
    for i in range(QCHUNKS):
        c = pltpu.make_async_copy(wt_hbm.at[pl.ds(i * qstep, qstep)], wq_v.at[pl.ds(i * qstep, qstep)], wq_sem.at[i])
        c.start()
        wq_copies.append(c)
    ostep = WIDTH // OCHUNKS
    wo_copies = []
    for i in range(OCHUNKS):
        c = pltpu.make_async_copy(wo_hbm.at[pl.ds(i * ostep, ostep)], wo_v.at[pl.ds(i * ostep, ostep)], wo_sem.at[i])
        c.start()
        wo_copies.append(c)

    barrier = pltpu.get_barrier_semaphore()
    for peer in (partner, xnbr, ynbr):
        pl.semaphore_signal(barrier, inc=1, device_id=peer, device_id_type=MESH)

    qp_v[...] = jnp.zeros_like(qp_v)
    x_copy.wait()
    xt_v[...] = x_v[...].T

    wkv_copies[0].wait()
    k_own = lax.dot_general(x_v[...], wkv_v[0], (((1,), (1,)), ((), ())), preferred_element_type=F32)
    k_v[0, pl.ds(0, TOK), :] = k_own.astype(BF16)
    wkv_copies[1].wait()
    vt_own = jnp.dot(wkv_v[1], xt_v[...], preferred_element_type=F32)
    vt_v[0, 0, :, :] = vt_own.astype(BF16)

    pl.semaphore_wait(barrier, 3)

    def kref(phase, half):
        return k_v.at[phase, pl.ds(half * TOK, TOK)]

    def vref(phase, half):
        return vt_v.at[phase, half]

    def send(idx, src, dst, peer):
        c = pltpu.make_async_remote_copy(src_ref=src, dst_ref=dst, send_sem=send_sem.at[idx], recv_sem=recv_sem.at[idx],
                                         device_id=peer, device_id_type=MESH)
        return c

    kx = send(0, kref(0, 0), kref(1, 0), xnbr)
    vx = send(1, vref(0, 0), vref(1, 0), xnbr)
    vy = send(2, vref(0, 0), vref(2, 0), ynbr)
    ky = send(3, kref(0, 0), kref(2, 0), ynbr)
    kp = send(4, kref(0, 0), kref(0, 1), partner)
    vp = send(5, vref(0, 0), vref(0, 1), partner)
    for c in (kx, vy, vx, ky, kp, vp):
        c.start()
    kdiag = send(6, kref(1, 0), kref(3, 0), ynbr)
    vdiag = send(7, vref(2, 0), vref(3, 0), xnbr)
    kxp = send(8, kref(1, 0), kref(1, 1), partner)
    vxp = send(9, vref(1, 0), vref(1, 1), partner)
    kyp = send(10, kref(2, 0), kref(2, 1), partner)
    vyp = send(11, vref(2, 0), vref(2, 1), partner)
    kdp = send(12, kref(3, 0), kref(3, 1), partner)
    vdp = send(13, vref(3, 0), vref(3, 1), partner)

    for i in range(QCHUNKS):
        wq_copies[i].wait()
        qt = jnp.dot(wq_v[pl.ds(i * qstep, qstep), :], xt_v[...], preferred_element_type=F32).astype(BF16)
        heads_per = qstep // HD
        for h in range(heads_per):
            head = i * heads_per + h
            g = head // (HEADS // KVH)
            qp_v[head // 2, pl.ds(g * HD, HD), pl.ds((head % 2) * TOK, TOK)] = qt[h * HD:(h + 1) * HD]

    def attend(phase, first):
        keys = k_v.at[phase]

        def body(j, _):
            g = j // (TILES // KVH)
            s = jnp.dot(keys[...], qp_v[j], preferred_element_type=F32)
            smax = jnp.max(s, axis=0, keepdims=True) * SCALE
            if first:
                m_new = smax
            else:
                m_old = m_v[j]
                m_new = jnp.maximum(m_old, smax)
                alpha = jnp.exp2(m_old - m_new)
            p = jnp.exp2(s * SCALE - m_new)
            psum = jnp.sum(p, axis=0, keepdims=True)
            pb = p.astype(BF16)
            row = pl.multiple_of(g * HD, HD)
            pv = jnp.dot(vt_v[phase, 0, pl.ds(row, HD), :], pb[:TOK], preferred_element_type=F32)
            pv = pv + jnp.dot(vt_v[phase, 1, pl.ds(row, HD), :], pb[TOK:], preferred_element_type=F32)
            m_v[j] = m_new
            if first:
                l_v[j] = psum
                o_v[j] = pv
            else:
                l_v[j] = l_v[j] * alpha + psum
                o_v[j] = o_v[j] * alpha + pv
            return 0

        lax.fori_loop(0, TILES, body, 0, unroll=2)

    kp.wait_recv()
    vp.wait_recv()
    attend(0, True)

    kx.wait_recv()
    kdiag.start()
    kxp.start()
    vy.wait_recv()
    vdiag.start()
    vyp.start()
    vx.wait_recv()
    vxp.start()
    ky.wait_recv()
    kyp.start()
    kxp.wait_recv()
    vxp.wait_recv()
    attend(1, False)
    kdiag.wait_recv()
    kdp.start()
    vdiag.wait_recv()
    vdp.start()
    kyp.wait_recv()
    vyp.wait_recv()
    attend(2, False)
    kdp.wait_recv()
    vdp.wait_recv()
    attend(3, False)

    for j in range(TILES):
        inv = 1.0 / l_v[j]
        on = (o_v[j] * inv).astype(BF16)
        for e in range(2):
            head = 2 * j + e
            ob_v[pl.ds(head * HD, HD), :] = on[:, e * TOK:(e + 1) * TOK]
    o_rows = ob_v[...].T

    for c in wo_copies:
        c.wait()
    y_v[...] = jnp.dot(o_rows, wo_v[...], preferred_element_type=F32).astype(BF16)
    y_copy = pltpu.make_async_copy(y_v, y_hbm.at[0], y_sem)
    y_copy.start()
    y_copy.wait()
    for c in (kx, vx, vy, ky, kp, vp, kdiag, vdiag, kxp, vxp, kyp, vyp, kdp, vdp):
        c.wait_send()


def solution(mesh):
    seq_spec = P("dp", ("cy", "cx", "core"))

    def local_layer(x_loc, w_qkv, w_out):
        wt = jnp.transpose(w_qkv, (1, 2, 0)).reshape(QROWS + 2 * NKV, WIDTH)
        wo = w_out.reshape(QROWS, WIDTH)
        any_spec = pl.BlockSpec(memory_space=pl.ANY)
        return pl.pallas_call(
            kernel,
            out_shape=jax.ShapeDtypeStruct((1, TOK, WIDTH), BF16),
            in_specs=[any_spec] * 3,
            out_specs=any_spec,
            scratch_shapes=[
                pltpu.VMEM((TOK, WIDTH), BF16),
                pltpu.VMEM((WIDTH, TOK), BF16),
                pltpu.VMEM((2, NKV, WIDTH), BF16),
                pltpu.VMEM((QROWS, WIDTH), BF16),
                pltpu.VMEM((QROWS, WIDTH), BF16),
                pltpu.VMEM((TILES, NKV, COLS), BF16),
                pltpu.VMEM((4, 2 * TOK, NKV), BF16),
                pltpu.VMEM((4, 2, NKV, TOK), BF16),
                pltpu.VMEM((TILES, 1, COLS), F32),
                pltpu.VMEM((TILES, 1, COLS), F32),
                pltpu.VMEM((TILES, HD, COLS), F32),
                pltpu.VMEM((QROWS, TOK), BF16),
                pltpu.VMEM((TOK, WIDTH), BF16),
                pltpu.SemaphoreType.DMA,
                pltpu.SemaphoreType.DMA((2,)),
                pltpu.SemaphoreType.DMA((QCHUNKS,)),
                pltpu.SemaphoreType.DMA((OCHUNKS,)),
                pltpu.SemaphoreType.DMA,
                pltpu.SemaphoreType.DMA((14,)),
                pltpu.SemaphoreType.DMA((14,)),
            ],
            compiler_params=pltpu.CompilerParams(collective_id=0, has_side_effects=True, vmem_limit_bytes=60 * 1024 * 1024),
        )(x_loc, wt, wo)

    return jax.shard_map(local_layer, mesh=mesh, in_specs=(seq_spec, P(), P()), out_specs=seq_spec, check_vma=False)
```

time: 69.9 us -> 41.7 us (0.60)
  Pallas kernels: 0 us -> 39.6 us
  blocking collectives: 39.4 us -> 0 us
  matrix products: 16.9 us -> 0 us
  local copies, waits for them, and re-layouts: 10 us -> 1.88 us
  other arithmetic: 3.06 us -> 0 us
    pallas_call x0 -> x1, Pallas kernels: none -> 39.6 us  [local_layer(): pl.pallas_call(kernel, out_shape=jax.ShapeDtypeStruct((1, TOK, WIDTH), BF...]
    all_to_all x4 -> x0, blocking collectives: 33.2 us -> none  [the longest x1 13.8 us: local_layer(): packed = lax.all_to_all(packed, 'cx', 1, 0, tiled=True)]
    dot_general x5 -> x0, matrix products: 11.3 us -> none  [the longest x1 5.47 us: local_layer(): jnp.einsum('shd,hdc->sc', attn_out, w_out, preferred_element_type=jnp.flo...]
    all_gather x1 -> x0, blocking collectives: 6.2 us -> none  [local_layer(): kv_all = lax.all_gather(packed[:, 0, q_local:], 'cy')]
    unnamed x1 -> x0, matrix products: 5.61 us -> none
    all_to_all x7 -> x0, local copies, waits for them, and re-layouts: 4.45 us -> none  [the longest x2 2.34 us: local_layer(): attn_out = lax.all_to_all(attn_out, 'core', 0, 1, tiled=True)]
    reduce_sum x1 -> x0, other arithmetic: 2.85 us -> none  [local_layer(): run_sum = run_sum * rescale + weights.sum(axis=-1)]
    unnamed x6 -> x1, local copies, waits for them, and re-layouts: 4.16 us -> 1.88 us
where the time goes in v1:
time: 41.7 us; the launch traced here: 41.5 us
  Pallas kernels  39.6 us (95%)
  local copies, waits for them, and re-layouts  1.88 us (5%)
    pallas_call x1, Pallas kernels, local_layer(): pl.pallas_call(kernel, out_shape=jax.ShapeDtypeStruct((1, TOK, WIDTH), BF...  39.6 us
    unnamed x1, local copies, waits for them, and re-layouts  1.88 us

profile of v1, /device:TPU:0, one launch (start us, length us, event | category | flops | bytes accessed | tf_op | source)
XLA Modules:
  0.0 41.5 jit_solution(6872844159595127434)
XLA Ops:
  0.0 39.6 %shard_map.37 = bf16[1,128,2048]{2,1,0:T(8,128)(2,1)} custom-call(bf16[1,128,2048]{2,1,0:T(8,128)(2,1)} %x_hbm.1, bf16[2560,2048]{1,0:T(8,128)(2,1)} %bitcast.4, bf16[2048,2048]{1,0:T(8,128)(2,1)} %bitcast.5), custom_call_target="tpu_custom_call" | custom-call | tf_op jit(solution)/shard_map/pallas_call | solution.py:196
  39.6 1.9 %copy.5 = bf16[1,128,2048]{2,1,0:T(8,128)(2,1)} copy(bf16[1,128,2048]{2,1,0:T(8,128)(2,1)} %shard_map.37) | data formatting | bytes 1048576

commit v2 on v1

v2 whole, which is shorter than its diff:
```python
import functools
import math

import jax
import jax.numpy as jnp
from jax import lax
from jax.experimental import pallas as pl
from jax.experimental.pallas import tpu as pltpu
from jax.sharding import PartitionSpec as P

MESH = pl.DeviceIdType.MESH
F32 = jnp.float32
BF16 = jnp.bfloat16

TOK = 128
WIDTH = 2048
HEADS = 32
KVH = 4
HD = 64
NKV = KVH * HD
QROWS = HEADS * HD
TILES = HEADS // 2
COLS = 2 * TOK
QCHUNKS = 4
OCHUNKS = 4
NS = 3
NP = 3
SCALE = (HD ** -0.5) * math.log2(math.e)


def kernel(x_hbm, wt_hbm, wo_hbm, y_ref,
           x_v, xt_v, wkv_v, wq_v, wo_v, qp_v, k_v, vt_v, s_v, mp_v, p_v, m_v, al_v, l_v, o_v, ob_v,
           x_sem, wkv_sem, wq_sem, wo_sem, send_sem, recv_sem):
    cy = lax.axis_index("cy")
    cx = lax.axis_index("cx")
    co = lax.axis_index("core")
    partner = {"core": 1 - co}
    xnbr = {"cx": 1 - cx}
    ynbr = {"cy": 1 - cy}

    x_copy = pltpu.make_async_copy(x_hbm.at[0], x_v, x_sem)
    x_copy.start()
    wkv_copies = []
    for i in range(2):
        c = pltpu.make_async_copy(wt_hbm.at[pl.ds(QROWS + i * NKV, NKV)], wkv_v.at[i], wkv_sem.at[i])
        c.start()
        wkv_copies.append(c)

    barrier = pltpu.get_barrier_semaphore()
    for peer in (partner, xnbr, ynbr):
        pl.semaphore_signal(barrier, inc=1, device_id=peer, device_id_type=MESH)

    qstep = QROWS // QCHUNKS
    wq_copies = []
    for i in range(QCHUNKS):
        c = pltpu.make_async_copy(wt_hbm.at[pl.ds(i * qstep, qstep)], wq_v.at[pl.ds(i * qstep, qstep)], wq_sem.at[i])
        c.start()
        wq_copies.append(c)

    qp_v[...] = jnp.zeros_like(qp_v)
    x_copy.wait()
    xt_v[...] = x_v[...].T

    wkv_copies[0].wait()
    k_own = lax.dot_general(x_v[...], wkv_v[0], (((1,), (1,)), ((), ())), preferred_element_type=F32)
    k_v[pl.ds(0, TOK), :] = k_own.astype(BF16)
    wkv_copies[1].wait()
    v_own = lax.dot_general(x_v[...], wkv_v[1], (((1,), (1,)), ((), ())), preferred_element_type=F32)
    vt_v[:, pl.ds(0, TOK)] = v_own.astype(BF16).T

    pl.semaphore_wait(barrier, 3)

    def kref(slot):
        return k_v.at[pl.ds(slot * TOK, TOK)]

    def vref(slot):
        return vt_v.at[:, pl.ds(slot * TOK, TOK)]

    def send(idx, src, dst, peer):
        return pltpu.make_async_remote_copy(src_ref=src, dst_ref=dst, send_sem=send_sem.at[idx], recv_sem=recv_sem.at[idx],
                                            device_id=peer, device_id_type=MESH)

    kx = send(0, kref(0), kref(2), xnbr)
    vx = send(1, vref(0), vref(2), xnbr)
    vy = send(2, vref(0), vref(4), ynbr)
    ky = send(3, kref(0), kref(4), ynbr)
    kp = send(4, kref(0), kref(1), partner)
    vp = send(5, vref(0), vref(1), partner)
    for c in (kx, vy, vx, ky, kp, vp):
        c.start()
    kdiag = send(6, kref(2), kref(6), ynbr)
    vdiag = send(7, vref(4), vref(6), xnbr)
    kxp = send(8, kref(2), kref(3), partner)
    vxp = send(9, vref(2), vref(3), partner)
    kyp = send(10, kref(4), kref(5), partner)
    vyp = send(11, vref(4), vref(5), partner)
    kdp = send(12, kref(6), kref(7), partner)
    vdp = send(13, vref(6), vref(7), partner)

    ostep = WIDTH // OCHUNKS
    wo_copies = []
    for i in range(QCHUNKS):
        wq_copies[i].wait()
        if i == QCHUNKS - 1:
            for o in range(OCHUNKS):
                c = pltpu.make_async_copy(wo_hbm.at[pl.ds(o * ostep, ostep)], wo_v.at[pl.ds(o * ostep, ostep)], wo_sem.at[o])
                c.start()
                wo_copies.append(c)
        qt = jnp.dot(wq_v[pl.ds(i * qstep, qstep), :], xt_v[...], preferred_element_type=F32).astype(BF16)
        heads_per = qstep // HD
        for h in range(heads_per):
            head = i * heads_per + h
            g = head // (HEADS // KVH)
            qp_v[head // 2, pl.ds(g * HD, HD), pl.ds((head % 2) * TOK, TOK)] = qt[h * HD:(h + 1) * HD]

    def attend(slot, nk, first):
        k0 = slot * TOK

        def scores(j):
            s = jnp.dot(k_v[pl.ds(k0, nk), :], qp_v[j], preferred_element_type=F32)
            s_v[j % NS, pl.ds(0, nk), :] = s
            mp_v[j % NS] = jnp.max(s.reshape(nk // 8, 8, COLS), axis=0)

        def soft(j):
            m_new = jnp.max(mp_v[j % NS], axis=0, keepdims=True) * SCALE
            if not first:
                m_old = m_v[j]
                m_new = jnp.maximum(m_old, m_new)
                alpha = jnp.exp2(m_old - m_new)
                al_v[j] = alpha
            m_v[j] = m_new
            p = jnp.exp2(s_v[j % NS, pl.ds(0, nk), :] * SCALE - m_new)
            psum = jnp.sum(p.reshape(nk // 8, 8, COLS), axis=0)
            l_v[j] = psum if first else l_v[j] * alpha + psum
            p_v[j % NP, pl.ds(0, nk), :] = p.astype(BF16)

        def mix(j):
            g = j // (TILES // KVH)
            pv = jnp.dot(vt_v[pl.ds(g * HD, HD), pl.ds(k0, nk)], p_v[j % NP, pl.ds(0, nk), :], preferred_element_type=F32)
            o_v[j] = pv if first else o_v[j] * al_v[j] + pv

        for t in range(TILES + 2):
            if t < TILES:
                scores(t)
            if 0 <= t - 1 < TILES:
                soft(t - 1)
            if 0 <= t - 2 < TILES:
                mix(t - 2)

    kp.wait_recv()
    vp.wait_recv()
    attend(0, 2 * TOK, True)

    kx.wait_recv()
    kdiag.start()
    kxp.start()
    vy.wait_recv()
    vdiag.start()
    vyp.start()
    vx.wait_recv()
    vxp.start()
    ky.wait_recv()
    kyp.start()
    kxp.wait_recv()
    vxp.wait_recv()
    kyp.wait_recv()
    vyp.wait_recv()
    attend(2, 4 * TOK, False)
    kdiag.wait_recv()
    kdp.start()
    vdiag.wait_recv()
    vdp.start()
    kdp.wait_recv()
    vdp.wait_recv()
    attend(6, 2 * TOK, False)

    for j in range(TILES):
        inv = 1.0 / jnp.sum(l_v[j], axis=0, keepdims=True)
        on = (o_v[j] * inv).astype(BF16)
        for e in range(2):
            head = 2 * j + e
            ob_v[pl.ds(head * HD, HD), :] = on[:, e * TOK:(e + 1) * TOK]
    o_rows = ob_v[...].T

    for c in wo_copies:
        c.wait()
    y_ref[0] = jnp.dot(o_rows, wo_v[...], preferred_element_type=F32).astype(BF16)
    for c in (kx, vx, vy, ky, kp, vp, kdiag, vdiag, kxp, vxp, kyp, vyp, kdp, vdp):
        c.wait_send()


def solution(mesh):
    seq_spec = P("dp", ("cy", "cx", "core"))

    def local_layer(x_loc, w_qkv, w_out):
        wt = jnp.transpose(w_qkv, (1, 2, 0)).reshape(QROWS + 2 * NKV, WIDTH)
        wo = w_out.reshape(QROWS, WIDTH)
        any_spec = pl.BlockSpec(memory_space=pl.ANY)
        return pl.pallas_call(
            kernel,
            out_shape=jax.ShapeDtypeStruct((1, TOK, WIDTH), BF16),
            in_specs=[any_spec] * 3,
            out_specs=pl.BlockSpec(memory_space=pltpu.VMEM),
            scratch_shapes=[
                pltpu.VMEM((TOK, WIDTH), BF16),
                pltpu.VMEM((WIDTH, TOK), BF16),
                pltpu.VMEM((2, NKV, WIDTH), BF16),
                pltpu.VMEM((QROWS, WIDTH), BF16),
                pltpu.VMEM((QROWS, WIDTH), BF16),
                pltpu.VMEM((TILES, NKV, COLS), BF16),
                pltpu.VMEM((8 * TOK, NKV), BF16),
                pltpu.VMEM((NKV, 8 * TOK), BF16),
                pltpu.VMEM((NS, 4 * TOK, COLS), F32),
                pltpu.VMEM((NS, 8, COLS), F32),
                pltpu.VMEM((NP, 4 * TOK, COLS), BF16),
                pltpu.VMEM((TILES, 1, COLS), F32),
                pltpu.VMEM((TILES, 1, COLS), F32),
                pltpu.VMEM((TILES, 8, COLS), F32),
                pltpu.VMEM((TILES, HD, COLS), F32),
                pltpu.VMEM((QROWS, TOK), BF16),
                pltpu.SemaphoreType.DMA,
                pltpu.SemaphoreType.DMA((2,)),
                pltpu.SemaphoreType.DMA((QCHUNKS,)),
                pltpu.SemaphoreType.DMA((OCHUNKS,)),
                pltpu.SemaphoreType.DMA((14,)),
                pltpu.SemaphoreType.DMA((14,)),
            ],
            compiler_params=pltpu.CompilerParams(collective_id=0, has_side_effects=True, vmem_limit_bytes=60 * 1024 * 1024),
        )(x_loc, wt, wo)

    return jax.shard_map(local_layer, mesh=mesh, in_specs=(seq_spec, P(), P()), out_specs=seq_spec, check_vma=False)
```

time: 41.7 us -> 23 us (0.55)
  Pallas kernels: 39.6 us -> 21 us
    pallas_call x1, Pallas kernels: 39.6 us -> 21 us  [local_layer(): pl.pallas_call(kernel, out_shape=jax.ShapeDtypeStruct((1, TOK, WIDTH), BF...]
where the time goes in v2:
time: 23 us; the launch traced here: 22.9 us
  Pallas kernels  21 us (91%)
  local copies, waits for them, and re-layouts  1.88 us (8%)
    pallas_call x1, Pallas kernels, local_layer(): pl.pallas_call(kernel, out_shape=jax.ShapeDtypeStruct((1, TOK, WIDTH), BF...  21 us
    unnamed x1, local copies, waits for them, and re-layouts  1.88 us

profile of v2, /device:TPU:0, one launch (start us, length us, event | category | flops | bytes accessed | tf_op | source)
XLA Modules:
  0.0 22.9 jit_solution(14476437907837963731)
XLA Ops:
  0.0 21.0 %shard_map.37 = bf16[1,128,2048]{2,1,0:T(8,128)(2,1)} custom-call(bf16[1,128,2048]{2,1,0:T(8,128)(2,1)} %x_hbm.1, bf16[2560,2048]{1,0:T(8,128)(2,1)} %bitcast.4, bf16[2048,2048]{1,0:T(8,128)(2,1)} %bitcast.5), custom_call_target="tpu_custom_call" | custom-call | tf_op jit(solution)/shard_map/pallas_call | solution.py:199
  21.0 1.9 %copy.5 = bf16[1,128,2048]{2,1,0:T(8,128)(2,1)} copy(bf16[1,128,2048]{2,1,0:T(8,128)(2,1)} %shard_map.37) | data formatting | bytes 1048576
